TPU v7x, 8 devices: a whole 2x2x1 slice. The times are simulated.
8 devices in a mesh: nodes: 8 (over z, y, x, core).
Axes of the slice: x: 2, y: 2, z: 1, core: 2. Of those that a mesh axis runs over, the one named last changes fastest.
Arguments:
- adjacency: bfloat16 [16384, 16384], P('nodes')
- features: bfloat16 [16384, 602], P('nodes')
- w_one: float32 [602, 128], replicated
- w_two: float32 [128, 41], replicated
- labels: int32 [16384], P('nodes')
- label_mask: int32 [16384], P('nodes')
Outputs:
- output 1: float32 [], replicated
- output 2: float32 [602, 128], replicated
- output 3: float32 [128, 41], replicated
All inputs are finite; a program needn't handle non-finite values.
Results may differ from a plain program's by a relative error of at most 0.0021.
Values are sent between devices in bfloat16 or wider.
A program may use at most 1 GiB of HBM per device.

v0:
```python
import jax
import jax.numpy as jnp
from jax import lax
from jax.sharding import PartitionSpec as P


def contract_rows(left, right):
    return lax.dot_general(left, right, (((0,), (0,)), ((), ())), preferred_element_type=jnp.float32)


def solution(mesh):
    node_axis = mesh.axis_names[0]

    def local_step(adj_rows, feat_rows, w_one, w_two, label_rows, mask_rows):
        classes = w_two.shape[1]
        w_one_b = w_one.astype(jnp.bfloat16)
        w_two_b = w_two.astype(jnp.bfloat16)
        y_one = jnp.dot(feat_rows, w_one_b, preferred_element_type=jnp.float32).astype(jnp.bfloat16)
        y_one_all = lax.all_gather(y_one, node_axis, tiled=True)
        z_one = jnp.dot(adj_rows, y_one_all, preferred_element_type=jnp.float32)
        h_one = jnp.maximum(z_one, 0.0).astype(jnp.bfloat16)
        y_two = jnp.dot(h_one, w_two_b, preferred_element_type=jnp.float32).astype(jnp.bfloat16)
        y_two_all = lax.all_gather(y_two, node_axis, tiled=True)
        z_two = jnp.dot(adj_rows, y_two_all, preferred_element_type=jnp.float32)
        mask_f = mask_rows.astype(jnp.float32)
        label_count = lax.psum(jnp.sum(mask_f), node_axis)
        log_norm = jax.nn.logsumexp(z_two, axis=1)
        onehot = (label_rows[:, None] == jnp.arange(classes, dtype=jnp.int32)[None, :]).astype(jnp.float32)
        picked = jnp.sum(z_two * onehot, axis=1)
        loss_value = lax.psum(jnp.sum(mask_f * (log_norm - picked)), node_axis) / label_count
        soft_probs = jnp.exp(z_two - log_norm[:, None])
        g_two = ((soft_probs - onehot) * (mask_f / label_count)[:, None]).astype(jnp.bfloat16)
        part_y2 = contract_rows(adj_rows, g_two)
        grad_y2 = lax.psum_scatter(part_y2, node_axis, scatter_dimension=0, tiled=True).astype(jnp.bfloat16)
        grad_two = lax.psum(contract_rows(h_one, grad_y2), node_axis)
        grad_h1 = lax.dot_general(grad_y2, w_two_b, (((1,), (1,)), ((), ())), preferred_element_type=jnp.float32)
        grad_z1 = jnp.where(z_one > 0.0, grad_h1, 0.0).astype(jnp.bfloat16)
        part_y1 = contract_rows(adj_rows, grad_z1)
        grad_y1 = lax.psum_scatter(part_y1, node_axis, scatter_dimension=0, tiled=True).astype(jnp.bfloat16)
        grad_one = lax.psum(contract_rows(feat_rows, grad_y1), node_axis)
        return loss_value, grad_one, grad_two

    return jax.shard_map(local_step, mesh=mesh, in_specs=(P(node_axis, None), P(node_axis, None), P(None, None), P(None, None), P(node_axis), P(node_axis)), out_specs=(P(), P(None, None), P(None, None)), check_vma=False)
```

profile of v0, /device:TPU:0, one launch (start us, length us, event | category | flops | bytes accessed | tf_op | source)
XLA Modules:
  0.0 361.6 jit_solution(7182218548214045856)
XLA Ops:
  7.2 0.0 copy-start
  7.2 0.0 all-gather.3.cloned.1.call-start
  7.2 1.6 copy-done
  8.9 2.7 convolution_convert_fusion
  11.5 0.0 all-gather.3.cloned.1.call-update
  11.6 0.0 all-gather.5.cloned.1.call-start
  11.6 33.7 %all-gather.3.cloned.1.call-done = bf16[16384,128]{1,0:T(8,128)(2,1)} async-done(((bf16[2048,128]{1,0:T(8,128)(2,1)}), bf16[16384,128]{1,0:T(8,128)(2,1)}) %all-gather.3.cloned.1.call-update) | async-done | bytes 4194320 | tf_op jit(solution)/shard_map/all_gather | solution.py:19
  45.3 29.5 %fusion.29 = f32[128,2048]{1,0:T(8,128)S(1)} fusion(bf16[16384,128]{1,0:T(8,128)(2,1)} %all-gather.3.cloned.1.call-done, bf16[2048,16384]{1,0:T(8,128)(2,1)} %param.6), kind=kOutput, calls=%fused_computation.42 | convolution fusion | flops 8589934592 | bytes 72351744 | tf_op jit(solution)/shard_map/dot_general | solution.py:20
  74.8 1.6 convolution_convert_fusion.1
  76.4 0.0 all-gather.5.cloned.1.call-update
  76.4 0.0 copy-start.1
  76.5 0.0 reduce-scatter.3.cloned.1.call-start
  76.5 19.8 %all-gather.5.cloned.1.call-done = bf16[16384,41]{0,1:T(8,128)(2,1)} async-done(((bf16[2048,41]{0,1:T(8,128)(2,1)}), bf16[16384,41]{0,1:T(8,128)(2,1)}) %all-gather.5.cloned.1.call-update) | async-done | bytes 1343504 | tf_op jit(solution)/shard_map/all_gather | solution.py:23
  96.3 27.7 %fusion.28 = (f32[2048]{0:T(1024)S(1)}, f32[41,2048]{1,0:T(8,128)}) fusion(bf16[16384,41]{0,1:T(8,128)(2,1)} %all-gather.5.cloned.1.call-done, bf16[2048,16384]{1,0:T(8,128)(2,1)} %param.6), kind=kOutput, calls=%fused_computation.41 | convolution fusion | flops 2751545344 | bytes 68796416 | tf_op jit(solution)/shard_map/dot_general | solution.py:24
  124.0 0.0 copy-start.2
  124.1 0.0 copy-done.1
  124.1 1.1 fusion.8
  125.2 0.0 copy-done.2
  125.2 1.3 convert_reduce_fusion
  126.5 22.4 %psum.29 = f32[]{:T(128)} all-reduce(f32[]{:T(128)} %get-tuple-element.5), channel_id=1, replica_groups=mesh['nodes'=8] {'nodes'}, use_global_device_ids=true, to_apply=%region_6.0 | all-reduce | flops 1 | bytes 8 | tf_op jit(solution)/shard_map/psum | solution.py:26
  149.0 1.3 convert_divide_fusion
  150.3 26.2 %convolution_bitcast_fusion.1 = f32[16384,41]{0,1:T(8,128)} fusion(bf16[2048,16384]{1,0:T(8,128)(2,1)} %param.6, f32[41,2048]{1,0:T(8,128)} %get-tuple-element.11, f32[2048]{0:T(1024)S(1)} %convert_divide_fusion, f32[2048]{0:T(1024)S(1)} %get-tuple-element.9, s32[2048]{0:T(1024)} %param.10), kind=kOutput, calls=%fused_computation.1 | convolution fusion | flops 2751967232 | bytes 70156288 | tf_op jit(solution)/shard_map/dot_general | solution.py:8
  176.5 0.0 reduce-scatter.3.cloned.1.call-update
  176.6 0.2 reduce-scatter.5.cloned.1.call-start
  176.8 39.3 %reduce-scatter.3.cloned.1.call-done = f32[2048,41]{0,1:T(8,128)} async-done(((f32[16384,41]{0,1:T(8,128)}), f32[2048,41]{0,1:T(8,128)}) %reduce-scatter.3.cloned.1.call-update) | async-done | bytes 335888 | tf_op jit(solution)/shard_map/reduce_scatter | solution.py:34
  216.1 27.4 %convolution_bitcast_fusion = f32[16384,128]{0,1:T(8,128)} fusion(bf16[2048,16384]{1,0:T(8,128)(2,1)} %param.6, f32[128,2048]{1,0:T(8,128)S(1)} %fusion.29, f32[2048,41]{0,1:T(8,128)} %reduce-scatter.3.cloned.1.call-done, f32[128,41]{0,1:T(8,128)} %param.9), kind=kOutput, calls=%fused_computation | convolution fusion | flops 8612305920 | bytes 76902912 | tf_op jit(solution)/shard_map/dot_general | solution.py:8
  243.5 0.0 reduce-scatter.5.cloned.1.call-update
  243.5 0.0 all-reduce.3.cloned.1.call-start
  243.6 62.4 %reduce-scatter.5.cloned.1.call-done = f32[2048,128]{0,1:T(8,128)} async-done(((f32[16384,128]{0,1:T(8,128)}), f32[2048,128]{0,1:T(8,128)}) %reduce-scatter.5.cloned.1.call-update) | async-done | bytes 1048592 | tf_op jit(solution)/shard_map/reduce_scatter | solution.py:39
  305.9 2.8 convolution_bitcast_fusion.2
  308.7 0.0 all-reduce.3.cloned.1.call-update
  308.7 1.9 fusion.13
  310.6 23.1 %all-reduce = (f32[]{:T(128)}, f32[128,41]{0,1:T(8,128)}) all-reduce(f32[]{:T(128)} %get-tuple-element.6, f32[128,41]{0,1:T(8,128)} %fusion.13), channel_id=1, replica_groups=mesh['nodes'=8] {'nodes'}, use_global_device_ids=true, to_apply=%region_4.0 | all-reduce | flops 5249 | bytes 41992 | tf_op jit(solution)/shard_map/psum | solution.py:30
  335.1 17.2 %all-reduce.3.cloned.1.call-done = f32[602,128]{1,0:T(8,128)} async-done(((f32[602,128]{1,0:T(8,128)}), f32[602,128]{1,0:T(8,128)}) %all-reduce.3.cloned.1.call-update) | async-done | bytes 308240 | tf_op jit(solution)/shard_map/psum | solution.py:40
  352.2 1.7 copy.10
  (1 shorter events, 0.0 us)
Async XLA Ops:
  7.2 1.7 copy-start
  7.2 38.1 %all-gather.3.cloned.1.call-start = ((), (), s32[]{:S(2)}) async-start(), calls=%async_computation.2 | async-start | bytes 4718592 | tf_op jit(solution)/shard_map/all_gather | solution.py:19
  11.6 84.8 %all-gather.5.cloned.1.call-start = ((), (), s32[]{:S(2)}) async-start(), calls=%async_computation.3 | async-start | bytes 1769472 | tf_op jit(solution)/shard_map/all_gather | solution.py:23
  76.4 47.6 %copy-start.1 = (s32[2048]{0:T(1024)S(1)}, s32[2048]{0:T(1024)}, u32[]{:S(2)}) copy-start(s32[2048]{0:T(1024)} %param.10) | copy-start | bytes 24580
  76.5 139.7 %reduce-scatter.3.cloned.1.call-start = ((), (), s32[]{:S(2)}) async-start(), calls=%async_computation.4 | async-start | bytes 3538944 | tf_op jit(solution)/shard_map/reduce_scatter | solution.py:34
  124.0 1.1 copy-start.2
  176.6 129.4 %reduce-scatter.5.cloned.1.call-start = ((), (), s32[]{:S(2)}) async-start(), calls=%async_computation.5 | async-start | bytes 9437184 | tf_op jit(solution)/shard_map/reduce_scatter | solution.py:39
  243.5 108.7 %all-reduce.3.cloned.1.call-start = ((), (), s32[]{:S(2)}) async-start(), calls=%async_computation.6 | async-start | bytes 622592 | tf_op jit(solution)/shard_map/psum | solution.py:40
Sparse Core Ops, SparseCore 0:
  11.7 33.5 all-gather.2
  76.6 19.7 all-gather.4
  176.7 39.3 reduce-scatter.2
  243.6 62.2 reduce-scatter.4
  309.4 42.7 all-reduce.2
where the time goes:
time: 362 us
  waiting for transfers between devices  172 us (48%)
  matrix products  120 us (33%)
  blocking collectives  45.5 us (13%)
  between operations  16.3 us (5%)
  other arithmetic  3.82 us (1%)
    reduce_scatter x1, waiting for transfers between devices, local_step(): lax.psum_scatter(part_y1, node_axis, scatter_dimension=0, tiled=True)  62.4 us
    dot_general x4, matrix products, contract_rows(): lax.dot_general(left, right, (((0,), (0,)), ((), ())), preferred_element_...  58.3 us
    reduce_scatter x1, waiting for transfers between devices, local_step(): lax.psum_scatter(part_y2, node_axis, scatter_dimension=0, tiled=True)  39.3 us
    all_gather x1, waiting for transfers between devices, local_step(): y_one_all = lax.all_gather(y_one, node_axis, tiled=True)  33.7 us
    dot_general x1, matrix products, local_step(): z_one = jnp.dot(adj_rows, y_one_all, preferred_element_type=jnp.float32)  29.5 us
    dot_general x1, matrix products, local_step(): z_two = jnp.dot(adj_rows, y_two_all, preferred_element_type=jnp.float32)  27.7 us
    psum x1, blocking collectives, local_step(): lax.psum(jnp.sum(mask_f * (log_norm - picked)), node_axis) / label_count  23.1 us
    psum x1, blocking collectives, local_step(): label_count = lax.psum(jnp.sum(mask_f), node_axis)  22.4 us
  transfers between devices with their start and end apart: 5, of which 5 were waited for; matrix products, arithmetic and copies ran while one was open for 1% of the time, Pallas kernels for 0%

commit v1 on v0

--- a/solution.py
+++ b/solution.py
@@ -30,13 +30,13 @@
         loss_value = lax.psum(jnp.sum(mask_f * (log_norm - picked)), node_axis) / label_count
         soft_probs = jnp.exp(z_two - log_norm[:, None])
         g_two = ((soft_probs - onehot) * (mask_f / label_count)[:, None]).astype(jnp.bfloat16)
-        part_y2 = contract_rows(adj_rows, g_two)
-        grad_y2 = lax.psum_scatter(part_y2, node_axis, scatter_dimension=0, tiled=True).astype(jnp.bfloat16)
+        g_two_all = lax.all_gather(g_two, node_axis, tiled=True)
+        grad_y2 = jnp.dot(adj_rows, g_two_all, preferred_element_type=jnp.float32).astype(jnp.bfloat16)
         grad_two = lax.psum(contract_rows(h_one, grad_y2), node_axis)
         grad_h1 = lax.dot_general(grad_y2, w_two_b, (((1,), (1,)), ((), ())), preferred_element_type=jnp.float32)
         grad_z1 = jnp.where(z_one > 0.0, grad_h1, 0.0).astype(jnp.bfloat16)
-        part_y1 = contract_rows(adj_rows, grad_z1)
-        grad_y1 = lax.psum_scatter(part_y1, node_axis, scatter_dimension=0, tiled=True).astype(jnp.bfloat16)
+        grad_z1_all = lax.all_gather(grad_z1, node_axis, tiled=True)
+        grad_y1 = jnp.dot(adj_rows, grad_z1_all, preferred_element_type=jnp.float32).astype(jnp.bfloat16)
         grad_one = lax.psum(contract_rows(feat_rows, grad_y1), node_axis)
         return loss_value, grad_one, grad_two
 

time: 362 us -> 320 us (0.88)
  waiting for transfers between devices: 172 us -> 123 us
  matrix products: 120 us -> 126 us
    reduce_scatter x2 -> x0, waiting for transfers between devices: 102 us -> none  [the longest x1 62.4 us: local_step(): lax.psum_scatter(part_y1, node_axis, scatter_dimension=0, tiled=True)]
    all_gather x0 -> x2, waiting for transfers between devices: none -> 52.6 us  [the longest x1 30.8 us: local_step(): grad_z1_all = lax.all_gather(grad_z1, node_axis, tiled=True)]
    dot_general x0 -> x2, matrix products: none -> 29.7 us  [the longest x1 27.6 us: local_step(): jnp.dot(adj_rows, g_two_all, preferred_element_type=jnp.float32)]
    dot_general x4 -> x2, matrix products: 58.3 us -> 34.5 us  [contract_rows(): lax.dot_general(left, right, (((0,), (0,)), ((), ())), preferred_element_...]
where the time goes in v1:
time: 320 us; the launch traced here: 319 us
  matrix products  126 us (39%)
  waiting for transfers between devices  123 us (38%)
  blocking collectives  45.5 us (14%)
  between operations  16.3 us (5%)
  other arithmetic  5.57 us (2%)
  local copies, waits for them, and re-layouts  3.37 us (1%)
    dot_general x2, matrix products, contract_rows(): lax.dot_general(left, right, (((0,), (0,)), ((), ())), preferred_element_...  34.5 us
    all_gather x1, waiting for transfers between devices, local_step(): y_one_all = lax.all_gather(y_one, node_axis, tiled=True)  33.7 us
    all_gather x1, waiting for transfers between devices, local_step(): grad_z1_all = lax.all_gather(grad_z1, node_axis, tiled=True)  30.8 us
    dot_general x1, matrix products, local_step(): z_one = jnp.dot(adj_rows, y_one_all, preferred_element_type=jnp.float32)  29.5 us
    dot_general x1, matrix products, local_step(): z_two = jnp.dot(adj_rows, y_two_all, preferred_element_type=jnp.float32)  27.7 us
    dot_general x1, matrix products, local_step(): jnp.dot(adj_rows, g_two_all, preferred_element_type=jnp.float32)  27.6 us
    psum x1, blocking collectives, local_step(): lax.psum(jnp.sum(mask_f * (log_norm - picked)), node_axis) / label_count  23.1 us
    psum x1, blocking collectives, local_step(): label_count = lax.psum(jnp.sum(mask_f), node_axis)  22.4 us
  transfers between devices with their start and end apart: 5, of which 5 were waited for; matrix products, arithmetic and copies ran while one was open for 1% of the time, Pallas kernels for 0%

profile of v1, /device:TPU:0, one launch (start us, length us, event | category | flops | bytes accessed | tf_op | source)
XLA Modules:
  0.0 319.5 jit_solution(3582437052335566808)
XLA Ops:
  7.2 0.0 copy-start
  7.2 0.0 all-gather.5.cloned.1.call-start
  7.2 1.6 copy-done
  8.9 2.7 convolution_convert_fusion
  11.6 0.0 all-gather.5.cloned.1.call-update
  11.6 0.0 all-gather.7.cloned.1.call-start
  11.6 33.7 %all-gather.5.cloned.1.call-done = bf16[16384,128]{1,0:T(8,128)(2,1)} async-done(((bf16[2048,128]{1,0:T(8,128)(2,1)}), bf16[16384,128]{1,0:T(8,128)(2,1)}) %all-gather.5.cloned.1.call-update) | async-done | bytes 4194320 | tf_op jit(solution)/shard_map/all_gather | solution.py:19
  45.3 29.5 %fusion.17 = f32[128,2048]{1,0:T(8,128)S(1)} fusion(bf16[16384,128]{1,0:T(8,128)(2,1)} %all-gather.5.cloned.1.call-done, bf16[2048,16384]{1,0:T(8,128)(2,1)} %param.6), kind=kOutput, calls=%fused_computation.32 | convolution fusion | flops 8589934592 | bytes 72351744 | tf_op jit(solution)/shard_map/dot_general | solution.py:20
  74.8 1.6 convolution_convert_fusion.3
  76.4 0.0 all-gather.7.cloned.1.call-update
  76.4 0.0 copy-start.1
  76.5 0.0 all-gather.9.cloned.1.call-start
  76.5 19.8 %all-gather.7.cloned.1.call-done = bf16[16384,41]{0,1:T(8,128)(2,1)} async-done(((bf16[2048,41]{0,1:T(8,128)(2,1)}), bf16[16384,41]{0,1:T(8,128)(2,1)}) %all-gather.7.cloned.1.call-update) | async-done | bytes 1343504 | tf_op jit(solution)/shard_map/all_gather | solution.py:23
  96.3 27.7 %fusion.16 = (f32[2048]{0:T(1024)S(1)}, f32[41,2048]{1,0:T(8,128)}) fusion(bf16[16384,41]{0,1:T(8,128)(2,1)} %all-gather.7.cloned.1.call-done, bf16[2048,16384]{1,0:T(8,128)(2,1)} %param.6), kind=kOutput, calls=%fused_computation.31 | convolution fusion | flops 2751545344 | bytes 68796416 | tf_op jit(solution)/shard_map/dot_general | solution.py:24
  124.0 0.0 copy-done.1
  124.0 1.1 fusion.5
  125.2 1.3 convert_reduce_fusion
  126.5 22.4 %psum.29 = f32[]{:T(128)} all-reduce(f32[]{:T(128)} %get-tuple-element.5), channel_id=1, replica_groups=mesh['nodes'=8] {'nodes'}, use_global_device_ids=true, to_apply=%region_6.0 | all-reduce | flops 1 | bytes 8 | tf_op jit(solution)/shard_map/psum | solution.py:26
  148.9 1.3 convert_divide_fusion
  150.3 1.8 fusion.9
  152.0 0.0 all-gather.9.cloned.1.call-update
  152.1 0.0 all-gather.11.cloned.1.call-start
  152.1 21.8 %all-gather.9.cloned.1.call-done = bf16[16384,41]{0,1:T(8,128)(2,1)} async-done(((bf16[2048,41]{0,1:T(8,128)(2,1)}), bf16[16384,41]{0,1:T(8,128)(2,1)}) %all-gather.9.cloned.1.call-update) | async-done | bytes 1343504 | tf_op jit(solution)/shard_map/all_gather | solution.py:33
  173.9 27.6 %convolution_convert_fusion.2 = bf16[41,2048]{1,0:T(8,128)(2,1)} fusion(bf16[16384,41]{0,1:T(8,128)(2,1)} %all-gather.9.cloned.1.call-done, bf16[2048,16384]{1,0:T(8,128)(2,1)} %param.6), kind=kOutput, calls=%fused_computation.4 | convolution fusion | flops 2751547392 | bytes 68620288 | tf_op jit(solution)/shard_map/dot_general | solution.py:34
  201.5 2.1 fusion
  203.6 0.0 all-gather.11.cloned.1.call-update
  203.6 0.0 all-reduce.3.cloned.1.call-start
  203.6 30.8 %all-gather.11.cloned.1.call-done = bf16[16384,128]{0,1:T(8,128)(2,1)} async-done(((bf16[2048,128]{0,1:T(8,128)(2,1)}), bf16[16384,128]{0,1:T(8,128)(2,1)}) %all-gather.11.cloned.1.call-update) | async-done | bytes 4194320 | tf_op jit(solution)/shard_map/all_gather | solution.py:38
  234.5 32.6 %fusion.2 = f32[602,128]{1,0:T(8,128)} fusion(bf16[2048,602]{0,1:T(8,128)(2,1)S(1)} %copy-done, bf16[16384,128]{0,1:T(8,128)(2,1)} %all-gather.11.cloned.1.call-done, bf16[2048,16384]{1,0:T(8,128)(2,1)} %param.6), kind=kOutput, calls=%fused_computation.7 | convolution fusion | flops 8905818112 | bytes 74077184 | tf_op jit(solution)/shard_map/dot_general | solution.py:8
  267.1 0.0 all-reduce.3.cloned.1.call-update
  267.2 1.8 fusion.10
  269.0 23.1 %all-reduce = (f32[]{:T(128)}, f32[128,41]{0,1:T(8,128)}) all-reduce(f32[]{:T(128)} %get-tuple-element.6, f32[128,41]{0,1:T(8,128)} %fusion.10), channel_id=1, replica_groups=mesh['nodes'=8] {'nodes'}, use_global_device_ids=true, to_apply=%region_4.0 | all-reduce | flops 5249 | bytes 41992 | tf_op jit(solution)/shard_map/psum | solution.py:30
  293.4 16.7 %all-reduce.3.cloned.1.call-done = f32[602,128]{1,0:T(8,128)} async-done(((f32[602,128]{1,0:T(8,128)}), f32[602,128]{1,0:T(8,128)}) %all-reduce.3.cloned.1.call-update) | async-done | bytes 308240 | tf_op jit(solution)/shard_map/psum | solution.py:40
  310.1 1.7 copy.10
  (1 shorter events, 0.0 us)
Async XLA Ops:
  7.2 1.7 copy-start
  7.2 38.1 %all-gather.5.cloned.1.call-start = ((), (), s32[]{:S(2)}) async-start(), calls=%async_computation | async-start | bytes 4718592 | tf_op jit(solution)/shard_map/all_gather | solution.py:19
  11.6 84.8 %all-gather.7.cloned.1.call-start = ((), (), s32[]{:S(2)}) async-start(), calls=%async_computation.1 | async-start | bytes 1769472 | tf_op jit(solution)/shard_map/all_gather | solution.py:23
  76.4 47.6 %copy-start.1 = (s32[2048]{0:T(1024)S(1)}, s32[2048]{0:T(1024)}, u32[]{:S(2)}) copy-start(s32[2048]{0:T(1024)} %param.10) | copy-start | bytes 24580
  76.5 97.4 %all-gather.9.cloned.1.call-start = ((), (), s32[]{:S(2)}) async-start(), calls=%async_computation.2 | async-start | bytes 1769472 | tf_op jit(solution)/shard_map/all_gather | solution.py:33
  152.1 82.4 %all-gather.11.cloned.1.call-start = ((), (), s32[]{:S(2)}) async-start(), calls=%async_computation.3 | async-start | bytes 4718592 | tf_op jit(solution)/shard_map/all_gather | solution.py:38
  203.6 106.5 %all-reduce.3.cloned.1.call-start = ((), (), s32[]{:S(2)}) async-start(), calls=%async_computation.4 | async-start | bytes 622592 | tf_op jit(solution)/shard_map/psum | solution.py:40
Sparse Core Ops, SparseCore 0:
  11.7 33.5 all-gather.4
  76.6 19.7 all-gather.6
  152.2 21.6 all-gather.8
  203.7 30.7 all-gather.10
  267.3 42.7 all-reduce.2

commit v2 on v1

v2 whole, which is shorter than its diff:
```python
import functools

import jax
import jax.numpy as jnp
from jax import lax
from jax.experimental import pallas as pl
from jax.experimental.pallas import tpu as pltpu
from jax.sharding import PartitionSpec as P

BF = jnp.bfloat16
F32 = jnp.float32
MESH = pl.DeviceIdType.MESH
NB = 3
XS, YS, XO, YO, ZS, ZO = range(6)


def dot_nn(a, b):
    return lax.dot_general(a, b, (((1,), (0,)), ((), ())), preferred_element_type=F32)


def dot_nt(a, b):
    return lax.dot_general(a, b, (((1,), (1,)), ((), ())), preferred_element_type=F32)


def kernel(dims, adj, feat, w1_ref, w2_ref, lab_ref, msk_ref, out_ref,
           ring, res, wide, thin, accs, precv, precv_thin, xbuf, h1, cnt_s, cnt_r, w2p,
           fin, fr1, half, fr2, fin_all,
           ring_sem, res_sem, x_sem, g_send, g_recv, p_send, p_recv, c_send, c_recv, f_send, f_recv):
    rows, width, hidden, classes = dims
    cpad = thin.shape[3]
    nch = 4
    ck = rows // nch
    me = lax.axis_index("nodes")
    core = lax.rem(me, 2)
    chip = me // 2
    xc = chip + 1 - 2 * lax.rem(chip, 2)
    yc = lax.rem(chip + 2, 4)
    zc = 3 - chip
    other = 1 - core
    part = chip * 2 + other
    xs, xo, ys, yo, zs, zo = (xc * 2 + core, xc * 2 + other, yc * 2 + core, yc * 2 + other,
                              zc * 2 + core, zc * 2 + other)
    dev_of = (xs, ys, xo, yo, zs, zo)

    def ring_copy(t):
        m = lax.rem(t, 12)
        b, q = m // 4, lax.rem(m, 4)
        e = ((1 - b) * (2 - b) // 2) * me + b * (2 - b) * part + (b * (b - 1) // 2) * zo
        slot = lax.rem(t, NB)
        cols = pl.ds(pl.multiple_of(e * rows + q * ck, ck), ck)
        return pltpu.make_async_copy(adj.at[:, cols], ring.at[slot], ring_sem.at[slot])

    def res_copy(r, q):
        cols = pl.ds(pl.multiple_of(dev_of[r] * rows + q * ck, ck), ck)
        return pltpu.make_async_copy(adj.at[:, cols], res.at[r * 4 + q], res_sem.at[r * 4 + q])

    x_copy = pltpu.make_async_copy(feat, xbuf, x_sem)
    x_copy.start()
    for t in range(NB):
        ring_copy(t).start()
    for q in range(nch):
        for r in (XS, YS, XO, YO):
            res_copy(r, q).start()
    for q in range(nch):
        res_copy(ZS, q).start()

    barrier = pltpu.get_barrier_semaphore()
    for o in range(1, 8):
        pl.semaphore_signal(barrier, inc=1, device_id=(lax.rem(me + o, 8),), device_id_type=MESH)

    mask_f = msk_ref[...].astype(F32)
    cnt_s[...] = jnp.broadcast_to(jnp.sum(mask_f, axis=1, keepdims=True), (8, 128))
    w1t = w1_ref[...].astype(BF).T
    w2p[...] = jnp.zeros_like(w2p)
    w2p[:, pl.ds(0, classes)] = w2_ref[...]
    w2b = w2p[:, pl.ds(0, cpad)].astype(BF)
    w2t = w2p[...].T[:cpad].astype(BF)
    pl.semaphore_wait(barrier, 7)

    def cnt_copy(o):
        return pltpu.make_async_remote_copy(cnt_s, cnt_r.at[o], c_send.at[o], c_recv.at[o],
                                            device_id=(lax.rem(me + o, 8),), device_id_type=MESH)

    def rdma(src, dst, ss, rs, dev):
        return pltpu.make_async_remote_copy(src, dst, ss, rs, device_id=(dev,), device_id_type=MESH)

    def gather_send(pi, buf):
        for q in range(nch):
            rdma(buf.at[me, q], buf.at[me, q], g_send.at[pi, 0, q], g_recv.at[pi, XS, q], xs).start()
            rdma(buf.at[me, q], buf.at[me, q], g_send.at[pi, 1, q], g_recv.at[pi, YS, q], ys).start()

    def run_pass(pi, n, buf, prv):
        gather_send(pi, buf)
        if pi == 0:
            for o in range(1, 8):
                cnt_copy(o).start()

        def local(m, _):
            t = pi * 12 + m
            b, q = m // 4, lax.rem(m, 4)
            ring_copy(t).wait()
            slot = lax.rem(t, NB)
            total = dot_nn(buf[me, 0], ring[slot, pl.ds(0, ck)])
            for c in range(1, nch):
                total += dot_nn(buf[me, c], ring[slot, pl.ds(c * ck, ck)])
            accs[b, pl.ds(0, n), pl.ds(pl.multiple_of(q * ck, ck), ck)] = total

            ring_copy(t + NB).start()
            return 0

        lax.fori_loop(0, 8, local, 0)
        p_copy = rdma(accs.at[1, pl.ds(0, n)], prv, p_send.at[pi], p_recv.at[pi], part)
        p_copy.start()

        def recv(r, q):
            return rdma(buf.at[dev_of[r], q], buf.at[dev_of[r], q], g_send.at[pi, 0, q], g_recv.at[pi, r, q], me)

        def relay(r, q):
            to = {XS: XO, YS: YO, ZS: ZO}[r]
            return rdma(buf.at[dev_of[r], q], buf.at[dev_of[r], q], g_send.at[pi, {XS: 2, YS: 3, ZS: 4}[r], q],
                        g_recv.at[pi, to, q], part)

        def forward(q, src, to):
            return rdma(buf.at[src, q], buf.at[src, q], g_send.at[pi, 5, q], g_recv.at[pi, ZS, q], to)

        def add(*terms):
            for i in range(nch):
                here = pl.ds(i * ck, ck)
                s = accs[0, pl.ds(0, n), here]
                for v, a in terms:
                    s += dot_nt(v, a[here, :])
                accs[0, pl.ds(0, n), here] = s

        def loaded(r, q):
            if pi == 0:
                res_copy(r, q).wait()
            return buf[dev_of[r], q], res.at[r * 4 + q]

        def near(q, _):
            recv(XS, q).wait_recv()
            relay(XS, q).start()

            @pl.when(q < 2)
            def _():
                forward(q, xs, ys).start()
            recv(YS, q).wait_recv()
            relay(YS, q).start()

            @pl.when(q >= 2)
            def _():
                forward(q, ys, xs).start()
            add(loaded(XS, q), loaded(YS, q))
            recv(XO, q).wait_recv()
            recv(YO, q).wait_recv()
            add(loaded(XO, q), loaded(YO, q))
            return 0

        lax.fori_loop(0, nch, near, 0)

        def far(q, _):
            recv(ZS, q).wait_recv()
            relay(ZS, q).start()
            add(loaded(ZS, q))
            t = pi * 12 + 8 + q
            ring_copy(t).wait()
            recv(ZO, q).wait_recv()
            add((buf[zo, q], ring.at[lax.rem(t, NB)]))

            if pi < 3:
                ring_copy(t + NB).start()
            else:
                @pl.when(q < nch - NB)
                def _():
                    ring_copy(t + NB).start()
            return 0

        lax.fori_loop(0, nch, far, 0)

        def drain(q, _):
            for i in range(6):
                rdma(buf.at[me, q], buf.at[me, q], g_send.at[pi, i, q], g_recv.at[pi, 0, q], me).wait_send()
            return 0

        lax.fori_loop(0, nch, drain, 0)
        p_copy.wait()

    x_copy.wait()
    for q in range(nch):
        wide[me, q] = dot_nt(w1t, xbuf[pl.ds(q * ck, ck)]).astype(BF)
    run_pass(0, hidden, wide, precv)

    for q in range(nch):
        here = pl.ds(q * ck, ck)
        h = jnp.maximum(accs[0, :, here] + precv[:, here], 0.0).astype(BF)
        h1[:, here] = h
        thin[0, me, q] = dot_nn(w2t, h).astype(BF)
    run_pass(1, cpad, thin.at[0], precv_thin.at[0])

    count = cnt_s[...]
    for o in range(1, 8):
        cnt_copy(o).wait()
        count += cnt_r[o]
    count = count[0:1, 0:1]
    loss_part = jnp.zeros((1, 1), F32)
    cls = lax.broadcasted_iota(jnp.int32, (cpad, ck), 0)
    real = cls < classes
    for q in range(nch):
        here = pl.ds(q * ck, ck)
        z2 = accs[0, pl.ds(0, cpad), here] + precv_thin[0, :, here]
        top = jnp.max(jnp.where(real, z2, -jnp.inf), axis=0, keepdims=True)
        total = jnp.sum(jnp.where(real, jnp.exp(z2 - top), 0.0), axis=0, keepdims=True)
        log_norm = top + jnp.log(total)
        hot = cls == lab_ref[:, here]
        picked = jnp.sum(jnp.where(hot, z2, 0.0), axis=0, keepdims=True)
        mask_f = msk_ref[:, here].astype(F32)
        loss_part += jnp.sum(mask_f * (log_norm - picked), axis=1, keepdims=True)
        soft = jnp.exp(z2 - log_norm)
        g2 = (soft - hot.astype(F32)) * (mask_f / count)
        thin[1, me, q] = jnp.where(real, g2, 0.0).astype(BF)
    run_pass(2, cpad, thin.at[1], precv_thin.at[1])

    d2 = jnp.zeros((hidden, cpad), F32)
    for q in range(nch):
        here = pl.ds(q * ck, ck)
        e2 = (accs[0, pl.ds(0, cpad), here] + precv_thin[1, :, here]).astype(BF)
        d2 += dot_nt(h1[:, here], e2)
        gh = dot_nn(w2b, e2)
        wide[me, q] = jnp.where(h1[:, here] > 0, gh, 0.0).astype(BF)
    col = lax.broadcasted_iota(jnp.int32, (hidden, cpad), 1)
    d2 = jnp.where(col == classes, loss_part / count, d2)
    run_pass(3, hidden, wide, precv)

    for q in range(nch):
        here = pl.ds(q * ck, ck)
        h1[:, here] = (accs[0, :, here] + precv[:, here]).astype(BF)
    fin[:, pl.ds(0, width)] = dot_nn(h1[...], xbuf[...])
    fin[:, pl.ds(width, fin.shape[1] - width)] = jnp.zeros((hidden, fin.shape[1] - width), F32)
    fin[:, pl.ds(fin.shape[1] - 128, cpad)] = d2

    hh, qq = hidden // 2, hidden // 8
    c0 = rdma(fin.at[pl.ds(pl.multiple_of(other * hh, hh), hh)], fr1, f_send.at[0], f_recv.at[0], part)
    c0.start()
    c0.wait()
    half[...] = fin[pl.ds(pl.multiple_of(core * hh, hh), hh)] + fr1[...]
    copies = []
    for i, (c, dev) in enumerate(((zc, zs), (xc, xs), (yc, ys))):
        cp = rdma(half.at[pl.ds(pl.multiple_of(c * qq, qq), qq)], fr2.at[i], f_send.at[1 + i], f_recv.at[1 + i], dev)
        cp.start()
        copies.append(cp)
    for cp in copies:
        cp.wait()
    mine = half[pl.ds(pl.multiple_of(chip * qq, qq), qq)] + (fr2[0] + fr2[1] + fr2[2])
    fin_all[me] = mine
    copies = []
    for i, dev in enumerate((zs, xs, ys, part)):
        cp = rdma(fin_all.at[me], fin_all.at[me], f_send.at[4 + i], f_recv.at[4 + i], dev)
        cp.start()
        copies.append(cp)
    back = []
    for i, dev in ((1, xs), (2, ys), (0, zs)):
        rdma(fin_all.at[dev], fin_all.at[dev], f_send.at[4 + i], f_recv.at[4 + i], me).wait_recv()
        cp = rdma(fin_all.at[dev], fin_all.at[dev], f_send.at[8 + i], f_recv.at[8 + i], part)
        cp.start()
        back.append(cp)
    rdma(fin_all.at[part], fin_all.at[part], f_send.at[7], f_recv.at[7], me).wait_recv()
    for i, dev in ((1, xo), (2, yo), (0, zo)):
        rdma(fin_all.at[dev], fin_all.at[dev], f_send.at[8 + i], f_recv.at[8 + i], me).wait_recv()
    for cp in copies + back:
        cp.wait_send()
    for d in range(8):
        out_ref[pl.ds((d % 2) * hh + (d // 2) * qq, qq)] = fin_all[d]


def solution(mesh):
    def local_step(adj_rows, feat_rows, w_one, w_two, label_rows, mask_rows):
        rows, nodes = adj_rows.shape
        width, hidden = w_one.shape
        classes = w_two.shape[1]
        cpad = (classes + 1 + 15) // 16 * 16
        ck = rows // 4
        fw = (width + 127) // 128 * 128 + 128
        dims = (rows, width, hidden, classes)
        vm = pl.BlockSpec(memory_space=pltpu.VMEM)
        hb = pl.BlockSpec(memory_space=pl.ANY)
        dma = pltpu.SemaphoreType.DMA
        with jax.named_scope("gcn"):
            out = pl.pallas_call(
                functools.partial(kernel, dims),
                out_shape=jax.ShapeDtypeStruct((hidden, fw), F32),
                in_specs=[hb, hb, vm, vm, vm, vm],
                out_specs=vm,
                scratch_shapes=[
                    pltpu.VMEM((NB, rows, ck), BF),
                    pltpu.VMEM((20, rows, ck), BF),
                    pltpu.VMEM((8, 4, hidden, ck), BF),
                    pltpu.VMEM((2, 8, 4, cpad, ck), BF),
                    pltpu.VMEM((2, hidden, rows), F32),
                    pltpu.VMEM((hidden, rows), F32),
                    pltpu.VMEM((2, cpad, rows), F32),
                    pltpu.VMEM((rows, width), BF),
                    pltpu.VMEM((hidden, rows), BF),
                    pltpu.VMEM((8, 128), F32),
                    pltpu.VMEM((8, 8, 128), F32),
                    pltpu.VMEM((hidden, 128), F32),
                    pltpu.VMEM((hidden, fw), F32),
                    pltpu.VMEM((hidden // 2, fw), F32),
                    pltpu.VMEM((hidden // 2, fw), F32),
                    pltpu.VMEM((3, hidden // 8, fw), F32),
                    pltpu.VMEM((8, hidden // 8, fw), F32),
                    dma((NB,)), dma((20,)), dma,
                    dma((4, 6, 4)), dma((4, 6, 4)), dma((4,)), dma((4,)), dma((8,)), dma((8,)), dma((11,)), dma((11,)),
                ],
                compiler_params=pltpu.CompilerParams(
                    collective_id=0, has_side_effects=True, vmem_limit_bytes=67043328
                ),
            )(adj_rows, feat_rows, w_one, w_two, label_rows.reshape(1, rows), mask_rows.reshape(1, rows))
        grad_one = out[:, :width].T
        return out[0, fw - 128 + classes], grad_one, out[:, fw - 128:fw - 128 + classes]

    ax = mesh.axis_names[0]
    return jax.shard_map(local_step, mesh=mesh, in_specs=(P(ax, None), P(ax, None), P(None, None), P(None, None), P(ax), P(ax)),
                         out_specs=(P(), P(None, None), P(None, None)), check_vma=False)
```

time: 320 us -> 144 us (0.45)
  Pallas kernels: 0 us -> 133 us
  matrix products: 126 us -> 0 us
  waiting for transfers between devices: 123 us -> 0 us
  blocking collectives: 45.5 us -> 0 us
  between operations: 16.3 us -> 0.64 us
  local copies, waits for them, and re-layouts: 3.37 us -> 10.5 us
  other arithmetic: 5.57 us -> 0 us
    pallas_call x0 -> x1, Pallas kernels: none -> 133 us  [local_step(): pl.pallas_call(functools.partial(kernel, dims), out_shape=jax.ShapeDtypeS...]
    dot_general x8 -> x0, matrix products: 126 us -> none  [the longest x2 34.5 us: contract_rows(): lax.dot_general(left, right, (((0,), (0,)), ((), ())), preferred_element_...]
    all_gather x4 -> x0, waiting for transfers between devices: 106 us -> none  [the longest x1 33.7 us: local_step(): y_one_all = lax.all_gather(y_one, node_axis, tiled=True)]
    psum x2 -> x0, blocking collectives: 45.5 us -> none  [the longest x1 23.1 us: local_step(): lax.psum(jnp.sum(mask_f * (log_norm - picked)), node_axis) / label_count]
    psum x1 -> x0, waiting for transfers between devices: 16.7 us -> none  [local_step(): grad_one = lax.psum(contract_rows(feat_rows, grad_y1), node_axis)]
    unnamed x5 -> x4, local copies, waits for them, and re-layouts: 3.37 us -> 7.39 us
  transfers between devices with their start and end apart: 5 -> 0, of which waited for: 5 -> 0; matrix products, arithmetic and copies ran while one was open for 1% -> 0% of each run, Pallas kernels for 0% -> 0%
where the time goes in v2:
time: 144 us
  Pallas kernels  133 us (92%)
  local copies, waits for them, and re-layouts  10.5 us (7%)
    pallas_call x1, Pallas kernels, local_step(): pl.pallas_call(functools.partial(kernel, dims), out_shape=jax.ShapeDtypeS...  133 us
    unnamed x4, local copies, waits for them, and re-layouts  7.39 us

profile of v2, /device:TPU:0, one launch (start us, length us, event | category | flops | bytes accessed | tf_op | source)
XLA Modules:
  0.0 143.8 jit_solution(11895871920334517998)
XLA Ops:
  0.6 1.5 %copy.10.w2_ref = f32[128,41]{1,0:T(8,128)} copy(f32[128,41]{0,1:T(8,128)} %param.9) | data formatting | bytes 41984 | tf_op args[3]
  2.1 4.4 %copy.9.feat = bf16[2048,602]{1,0:T(8,128)(2,1)} copy(bf16[2048,602]{0,1:T(8,128)(2,1)} %param.7) | data formatting | bytes 4931584 | tf_op args[1]
  6.5 132.6 %gcn.1 = f32[128,768]{1,0:T(8,128)} custom-call(bf16[2048,16384]{1,0:T(8,128)(2,1)} %adj.1, bf16[2048,602]{1,0:T(8,128)(2,1)} %copy.9.feat, f32[602,128]{1,0:T(8,128)} %w1_ref.1, f32[128,41]{1,0:T(8,128)} %copy.10.w2_ref, s32[1,2048]{1,0:T(1,128)} %bitcast.5, s32[1,2048]{1,0:T(1,128)} %bitcast.6), custom_call_target="tpu_custom_call" | custom-call | tf_op jit(solution)/shard_map/gcn/pallas_call | solution.py:287
  139.1 1.3 slice.9
  140.3 0.8 slice.11
  141.2 1.0 slice_bitcast_fusion
  142.2 0.7 copy.12
  142.9 0.9 copy.11

commit v3 on v2

--- a/solution.py
+++ b/solution.py
@@ -28,6 +28,7 @@
            ring_sem, res_sem, x_sem, g_send, g_recv, p_send, p_recv, c_send, c_recv, f_send, f_recv):
     rows, width, hidden, classes = dims
     cpad = thin.shape[3]
+    w8 = (width + 7) // 8 * 8
     nch = 4
     ck = rows // nch
     me = lax.axis_index("nodes")
@@ -72,9 +73,9 @@
     cnt_s[...] = jnp.broadcast_to(jnp.sum(mask_f, axis=1, keepdims=True), (8, 128))
     w1t = w1_ref[...].astype(BF).T
     w2p[...] = jnp.zeros_like(w2p)
-    w2p[:, pl.ds(0, classes)] = w2_ref[...]
-    w2b = w2p[:, pl.ds(0, cpad)].astype(BF)
-    w2t = w2p[...].T[:cpad].astype(BF)
+    w2p[pl.ds(0, classes)] = w2_ref[...]
+    w2t = w2p[pl.ds(0, cpad)].astype(BF)
+    w2b = w2p[...].T[:, :cpad].astype(BF)
     pl.semaphore_wait(barrier, 7)
 
     def cnt_copy(o):
@@ -186,7 +187,7 @@
 
     x_copy.wait()
     for q in range(nch):
-        wide[me, q] = dot_nt(w1t, xbuf[pl.ds(q * ck, ck)]).astype(BF)
+        wide[me, q] = dot_nn(w1t, xbuf[:, pl.ds(q * ck, ck)]).astype(BF)
     run_pass(0, hidden, wide, precv)
 
     for q in range(nch):
@@ -219,25 +220,24 @@
         thin[1, me, q] = jnp.where(real, g2, 0.0).astype(BF)
     run_pass(2, cpad, thin.at[1], precv_thin.at[1])
 
-    d2 = jnp.zeros((hidden, cpad), F32)
+    d2 = jnp.zeros((cpad, hidden), F32)
     for q in range(nch):
         here = pl.ds(q * ck, ck)
         e2 = (accs[0, pl.ds(0, cpad), here] + precv_thin[1, :, here]).astype(BF)
-        d2 += dot_nt(h1[:, here], e2)
+        d2 += dot_nt(e2, h1[:, here])
         gh = dot_nn(w2b, e2)
         wide[me, q] = jnp.where(h1[:, here] > 0, gh, 0.0).astype(BF)
-    col = lax.broadcasted_iota(jnp.int32, (hidden, cpad), 1)
-    d2 = jnp.where(col == classes, loss_part / count, d2)
+    row = lax.broadcasted_iota(jnp.int32, (cpad, hidden), 0)
+    fin[pl.ds(fin.shape[0] - hidden, hidden)] = jnp.zeros((hidden, hidden), F32)
+    fin[pl.ds(w8, cpad)] = jnp.where(row == classes, loss_part / count, d2)
     run_pass(3, hidden, wide, precv)
 
     for q in range(nch):
         here = pl.ds(q * ck, ck)
         h1[:, here] = (accs[0, :, here] + precv[:, here]).astype(BF)
-    fin[:, pl.ds(0, width)] = dot_nn(h1[...], xbuf[...])
-    fin[:, pl.ds(width, fin.shape[1] - width)] = jnp.zeros((hidden, fin.shape[1] - width), F32)
-    fin[:, pl.ds(fin.shape[1] - 128, cpad)] = d2
-
-    hh, qq = hidden // 2, hidden // 8
+    fin[pl.ds(0, width)] = dot_nt(xbuf[...], h1[...])
+
+    hh, qq = fin.shape[0] // 2, fin.shape[0] // 8
     c0 = rdma(fin.at[pl.ds(pl.multiple_of(other * hh, hh), hh)], fr1, f_send.at[0], f_recv.at[0], part)
     c0.start()
     c0.wait()
@@ -278,7 +278,8 @@
         classes = w_two.shape[1]
         cpad = (classes + 1 + 15) // 16 * 16
         ck = rows // 4
-        fw = (width + 127) // 128 * 128 + 128
+        w8 = (width + 7) // 8 * 8
+        fr = (w8 + cpad + 63) // 64 * 64
         dims = (rows, width, hidden, classes)
         vm = pl.BlockSpec(memory_space=pltpu.VMEM)
         hb = pl.BlockSpec(memory_space=pl.ANY)
@@ -286,7 +287,7 @@
         with jax.named_scope("gcn"):
             out = pl.pallas_call(
                 functools.partial(kernel, dims),
-                out_shape=jax.ShapeDtypeStruct((hidden, fw), F32),
+                out_shape=jax.ShapeDtypeStruct((fr, hidden), F32),
                 in_specs=[hb, hb, vm, vm, vm, vm],
                 out_specs=vm,
                 scratch_shapes=[
@@ -297,25 +298,24 @@
                     pltpu.VMEM((2, hidden, rows), F32),
                     pltpu.VMEM((hidden, rows), F32),
                     pltpu.VMEM((2, cpad, rows), F32),
-                    pltpu.VMEM((rows, width), BF),
+                    pltpu.VMEM((width, rows), BF),
                     pltpu.VMEM((hidden, rows), BF),
                     pltpu.VMEM((8, 128), F32),
                     pltpu.VMEM((8, 8, 128), F32),
                     pltpu.VMEM((hidden, 128), F32),
-                    pltpu.VMEM((hidden, fw), F32),
-                    pltpu.VMEM((hidden // 2, fw), F32),
-                    pltpu.VMEM((hidden // 2, fw), F32),
-                    pltpu.VMEM((3, hidden // 8, fw), F32),
-                    pltpu.VMEM((8, hidden // 8, fw), F32),
+                    pltpu.VMEM((fr, hidden), F32),
+                    pltpu.VMEM((fr // 2, hidden), F32),
+                    pltpu.VMEM((fr // 2, hidden), F32),
+                    pltpu.VMEM((3, fr // 8, hidden), F32),
+                    pltpu.VMEM((8, fr // 8, hidden), F32),
                     dma((NB,)), dma((20,)), dma,
                     dma((4, 6, 4)), dma((4, 6, 4)), dma((4,)), dma((4,)), dma((8,)), dma((8,)), dma((11,)), dma((11,)),
                 ],
                 compiler_params=pltpu.CompilerParams(
                     collective_id=0, has_side_effects=True, vmem_limit_bytes=67043328
                 ),
-            )(adj_rows, feat_rows, w_one, w_two, label_rows.reshape(1, rows), mask_rows.reshape(1, rows))
-        grad_one = out[:, :width].T
-        return out[0, fw - 128 + classes], grad_one, out[:, fw - 128:fw - 128 + classes]
+            )(adj_rows, feat_rows.T, w_one, w_two.T, label_rows.reshape(1, rows), mask_rows.reshape(1, rows))
+        return out[w8 + classes, 0], out[:width], out[w8:w8 + classes].T
 
     ax = mesh.axis_names[0]
     return jax.shard_map(local_step, mesh=mesh, in_specs=(P(ax, None), P(ax, None), P(None, None), P(None, None), P(ax), P(ax)),

time: 144 us -> 137 us (0.951)
  local copies, waits for them, and re-layouts: 10.5 us -> 4.24 us
    unnamed x4 -> x0, local copies, waits for them, and re-layouts: 7.39 us -> none
where the time goes in v3:
time: 137 us
  Pallas kernels  132 us (96%)
  local copies, waits for them, and re-layouts  4.24 us (3%)
    pallas_call x1, Pallas kernels, local_step(): pl.pallas_call(functools.partial(kernel, dims), out_shape=jax.ShapeDtypeS...  132 us
    slice x2, local copies, waits for them, and re-layouts, local_step(): return (out[w8 + classes, 0], out[:width], out[w8:w8 + classes].T)  2.89 us

profile of v3, /device:TPU:0, one launch (start us, length us, event | category | flops | bytes accessed | tf_op | source)
XLA Modules:
  0.0 137.0 jit_solution(12832096438931910458)
XLA Ops:
  0.6 132.1 %gcn.1 = f32[704,128]{1,0:T(8,128)} custom-call(bf16[2048,16384]{1,0:T(8,128)(2,1)} %adj.1, bf16[602,2048]{1,0:T(8,128)(2,1)} %bitcast.7, f32[602,128]{1,0:T(8,128)} %w1_ref.1, f32[41,128]{1,0:T(8,128)} %bitcast.8, s32[1,2048]{1,0:T(1,128)} %bitcast.9, s32[1,2048]{1,0:T(1,128)} %bitcast.10), custom_call_target="tpu_custom_call" | custom-call | tf_op jit(solution)/shard_map/gcn/pallas_call | solution.py:288
  132.7 1.2 slice.9
  133.9 1.3 slice_bitcast_fusion
  135.3 1.7 %slice.10 = f32[602,128]{1,0:T(8,128)} slice(f32[704,128]{1,0:T(8,128)} %gcn.1), slice={[0:602], [0:128]} | slice | bytes 616448 | tf_op jit(solution)/shard_map/slice | solution.py:318

commit v4 on v3

--- a/solution.py
+++ b/solution.py
@@ -10,7 +10,7 @@
 BF = jnp.bfloat16
 F32 = jnp.float32
 MESH = pl.DeviceIdType.MESH
-NB = 3
+NB = 4
 XS, YS, XO, YO, ZS, ZO = range(6)
 
 
@@ -22,12 +22,13 @@
     return lax.dot_general(a, b, (((1,), (1,)), ((), ())), preferred_element_type=F32)
 
 
-def kernel(dims, adj, feat, w1_ref, w2_ref, lab_ref, msk_ref, out_ref,
-           ring, res, wide, thin, accs, precv, precv_thin, xbuf, h1, cnt_s, cnt_r, w2p,
-           fin, fr1, half, fr2, fin_all,
-           ring_sem, res_sem, x_sem, g_send, g_recv, p_send, p_recv, c_send, c_recv, f_send, f_recv):
+def kernel(dims, adj, feat, tail_ref, w1_ref, w2_ref, lab_ref, msk_ref, out_ref,
+           ring, res, wide, thin, accs, precv, precv_thin, h1, cnt_s, cnt_r, w2p,
+           fin, fr1, fr2, fin_all,
+           ring_sem, x_sem, g_send, g_recv, p_send, p_recv, c_send, c_recv, f_send, f_recv):
     rows, width, hidden, classes = dims
     cpad = thin.shape[3]
+    whole = width // 8 * 8
     w8 = (width + 7) // 8 * 8
     nch = 4
     ck = rows // nch
@@ -43,27 +44,22 @@
                               zc * 2 + core, zc * 2 + other)
     dev_of = (xs, ys, xo, yo, zs, zo)
 
-    def ring_copy(t):
-        m = lax.rem(t, 12)
-        b, q = m // 4, lax.rem(m, 4)
-        e = ((1 - b) * (2 - b) // 2) * me + b * (2 - b) * part + (b * (b - 1) // 2) * zo
-        slot = lax.rem(t, NB)
+    def item(slot, e, q):
         cols = pl.ds(pl.multiple_of(e * rows + q * ck, ck), ck)
         return pltpu.make_async_copy(adj.at[:, cols], ring.at[slot], ring_sem.at[slot])
 
-    def res_copy(r, q):
-        cols = pl.ds(pl.multiple_of(dev_of[r] * rows + q * ck, ck), ck)
-        return pltpu.make_async_copy(adj.at[:, cols], res.at[r * 4 + q], res_sem.at[r * 4 + q])
-
-    x_copy = pltpu.make_async_copy(feat, xbuf, x_sem)
-    x_copy.start()
-    for t in range(NB):
-        ring_copy(t).start()
-    for q in range(nch):
-        for r in (XS, YS, XO, YO):
-            res_copy(r, q).start()
-    for q in range(nch):
-        res_copy(ZS, q).start()
+    def local_item(m):
+        return item(lax.rem(m, NB), me + (m // nch) * (part - me), lax.rem(m, nch))
+
+    near_dev = (xs, ys, xo, yo)
+
+    def x_copies(u):
+        more = whole - ck
+        return (pltpu.make_async_copy(feat.at[pl.ds(0, ck)], res.at[u], x_sem.at[0]),
+                pltpu.make_async_copy(feat.at[pl.ds(ck, more)], res.at[u + 1, pl.ds(0, more)], x_sem.at[1]))
+
+    for cp in x_copies(16):
+        cp.start()
 
     barrier = pltpu.get_barrier_semaphore()
     for o in range(1, 8):
@@ -76,6 +72,10 @@
     w2p[pl.ds(0, classes)] = w2_ref[...]
     w2t = w2p[pl.ds(0, cpad)].astype(BF)
     w2b = w2p[...].T[:, :cpad].astype(BF)
+    for cp in x_copies(16):
+        cp.wait()
+    for t in range(NB):
+        local_item(t).start()
     pl.semaphore_wait(barrier, 7)
 
     def cnt_copy(o):
@@ -92,26 +92,24 @@
 
     def run_pass(pi, n, buf, prv):
         gather_send(pi, buf)
+        if pi > 0:
+            accs[:, pl.ds(0, n)] = jnp.zeros((2, n, rows), F32)
         if pi == 0:
             for o in range(1, 8):
                 cnt_copy(o).start()
 
-        def local(m, _):
-            t = pi * 12 + m
-            b, q = m // 4, lax.rem(m, 4)
-            ring_copy(t).wait()
-            slot = lax.rem(t, NB)
+        def local_unit(m):
+            b, q = m // nch, lax.rem(m, nch)
+            slot = lax.rem(m, NB)
             total = dot_nn(buf[me, 0], ring[slot, pl.ds(0, ck)])
             for c in range(1, nch):
                 total += dot_nn(buf[me, c], ring[slot, pl.ds(c * ck, ck)])
-            accs[b, pl.ds(0, n), pl.ds(pl.multiple_of(q * ck, ck), ck)] = total
-
-            ring_copy(t + NB).start()
-            return 0
-
-        lax.fori_loop(0, 8, local, 0)
+            here = pl.ds(pl.multiple_of(q * ck, ck), ck)
+            if pi > 0:
+                total += accs[b, pl.ds(0, n), here]
+            accs[b, pl.ds(0, n), here] = total
+
         p_copy = rdma(accs.at[1, pl.ds(0, n)], prv, p_send.at[pi], p_recv.at[pi], part)
-        p_copy.start()
 
         def recv(r, q):
             return rdma(buf.at[dev_of[r], q], buf.at[dev_of[r], q], g_send.at[pi, 0, q], g_recv.at[pi, r, q], me)
@@ -124,20 +122,27 @@
         def forward(q, src, to):
             return rdma(buf.at[src, q], buf.at[src, q], g_send.at[pi, 5, q], g_recv.at[pi, ZS, q], to)
 
-        def add(*terms):
+        def add(*units):
             for i in range(nch):
                 here = pl.ds(i * ck, ck)
                 s = accs[0, pl.ds(0, n), here]
-                for v, a in terms:
-                    s += dot_nt(v, a[here, :])
+                for r, q in units:
+                    s += dot_nn(buf[dev_of[r], q], res[r * nch + q, :, here])
                 accs[0, pl.ds(0, n), here] = s
 
-        def loaded(r, q):
-            if pi == 0:
-                res_copy(r, q).wait()
-            return buf[dev_of[r], q], res.at[r * 4 + q]
-
-        def near(q, _):
+        def add_new(r, q, slot):
+            for i in range(nch):
+                here = pl.ds(i * ck, ck)
+                t = ring[slot, here, :].T
+                res[r * nch + q, :, here] = t
+                accs[0, pl.ds(0, n), here] += dot_nn(buf[dev_of[r], q], t)
+
+        def add_far(q, slot):
+            for i in range(nch):
+                here = pl.ds(i * ck, ck)
+                accs[0, pl.ds(0, n), here] += dot_nt(buf[zo, q], ring[slot, here, :])
+
+        def arrivals(q):
             recv(XS, q).wait_recv()
             relay(XS, q).start()
 
@@ -150,32 +155,123 @@
             @pl.when(q >= 2)
             def _():
                 forward(q, ys, xs).start()
-            add(loaded(XS, q), loaded(YS, q))
-            recv(XO, q).wait_recv()
-            recv(YO, q).wait_recv()
-            add(loaded(XO, q), loaded(YO, q))
-            return 0
-
-        lax.fori_loop(0, nch, near, 0)
-
-        def far(q, _):
+
+        def far_arrival(q):
             recv(ZS, q).wait_recv()
             relay(ZS, q).start()
-            add(loaded(ZS, q))
-            t = pi * 12 + 8 + q
-            ring_copy(t).wait()
-            recv(ZO, q).wait_recv()
-            add((buf[zo, q], ring.at[lax.rem(t, NB)]))
-
-            if pi < 3:
-                ring_copy(t + NB).start()
-            else:
-                @pl.when(q < nch - NB)
-                def _():
-                    ring_copy(t + NB).start()
-            return 0
-
-        lax.fori_loop(0, nch, far, 0)
+
+        if pi == 0:
+            def local(m, _):
+                local_item(m).wait()
+                local_unit(m)
+
+                @pl.when(m < 4)
+                def _():
+                    local_item(m + 4).start()
+                for j in range(4):
+                    @pl.when(m == 4 + j)
+                    def _(j=j):
+                        item(j, near_dev[j], 0).start()
+                return 0
+
+            lax.fori_loop(0, 8, local, 0)
+            p_copy.start()
+
+            def near(q, _):
+                arrivals(q)
+
+                @pl.when(q >= 2)
+                def _():
+                    far_arrival(q - 2)
+                for j, r in enumerate((XS, YS, XO, YO)):
+                    if j >= 2:
+                        recv(r, q).wait_recv()
+                    item(j, near_dev[j], q).wait()
+                    add_new(r, q, j)
+
+                    @pl.when(q < 3)
+                    def _(j=j):
+                        item(j, near_dev[j], q + 1).start()
+
+                    @pl.when(q == 3)
+                    def _(j=j):
+                        item(j, (zs, zo)[j % 2], j // 2).start()
+                return 0
+
+            lax.fori_loop(0, nch, near, 0)
+
+            def far(q, _):
+                @pl.when(q < 2)
+                def _():
+                    far_arrival(q + 2)
+                for j in range(2):
+                    slot = lax.rem(2 * q + j, NB)
+                    item(slot, (zs, zo)[j], q).wait()
+                    if j == 0:
+                        add_new(ZS, q, slot)
+                    else:
+                        recv(ZO, q).wait_recv()
+                        add_far(q, slot)
+
+                    @pl.when(q < 2)
+                    def _(j=j, slot=slot):
+                        item(slot, (zs, zo)[j], q + 2).start()
+
+                    @pl.when(q >= 2)
+                    def _(j=j):
+                        local_item(2 * (q - 2) + j).start()
+                return 0
+
+            lax.fori_loop(0, nch, far, 0)
+        else:
+            def near(q, _):
+                arrivals(q)
+
+                @pl.when(q >= 2)
+                def _():
+                    far_arrival(q - 2)
+                local_item(2 * q).wait()
+                local_item(2 * q + 1).wait()
+                local_unit(2 * q)
+                local_unit(2 * q + 1)
+
+                @pl.when(q < 2)
+                def _():
+                    local_item(2 * q + 4).start()
+                    local_item(2 * q + 5).start()
+
+                @pl.when(q >= 2)
+                def _():
+                    item(2 * q - 4, zo, 2 * q - 4).start()
+                    item(2 * q - 3, zo, 2 * q - 3).start()
+
+                @pl.when(q == 3)
+                def _():
+                    p_copy.start()
+                add((XS, q), (YS, q))
+                recv(XO, q).wait_recv()
+                recv(YO, q).wait_recv()
+                add((XO, q), (YO, q))
+                return 0
+
+            lax.fori_loop(0, nch, near, 0)
+            if pi == 3:
+                for cp in x_copies(0):
+                    cp.start()
+
+            def far(q, _):
+                @pl.when(q < 2)
+                def _():
+                    far_arrival(q + 2)
+                item(q, zo, q).wait()
+                recv(ZO, q).wait_recv()
+                add((ZS, q))
+                add_far(q, q)
+                if pi < 3:
+                    local_item(q).start()
+                return 0
+
+            lax.fori_loop(0, nch, far, 0)
 
         def drain(q, _):
             for i in range(6):
@@ -185,9 +281,12 @@
         lax.fori_loop(0, nch, drain, 0)
         p_copy.wait()
 
-    x_copy.wait()
     for q in range(nch):
-        wide[me, q] = dot_nn(w1t, xbuf[:, pl.ds(q * ck, ck)]).astype(BF)
+        here = pl.ds(q * ck, ck)
+        y1 = dot_nn(w1t[:, :ck], res[16, :, here])
+        y1 += dot_nn(w1t[:, ck:whole], res[17, pl.ds(0, whole - ck), here])
+        y1 += dot_nn(w1t[:, whole:], tail_ref[pl.ds(0, width - whole), here])
+        wide[me, q] = y1.astype(BF)
     run_pass(0, hidden, wide, precv)
 
     for q in range(nch):
@@ -235,13 +334,18 @@
     for q in range(nch):
         here = pl.ds(q * ck, ck)
         h1[:, here] = (accs[0, :, here] + precv[:, here]).astype(BF)
-    fin[pl.ds(0, width)] = dot_nt(xbuf[...], h1[...])
+    for cp in x_copies(0):
+        cp.wait()
+    fin[pl.ds(0, ck)] = dot_nt(res[0], h1[...])
+    fin[pl.ds(ck, whole - ck)] = dot_nt(res[1, pl.ds(0, whole - ck)], h1[...])
+    fin[pl.ds(whole, 8)] = dot_nt(tail_ref[...], h1[...])
 
     hh, qq = fin.shape[0] // 2, fin.shape[0] // 8
     c0 = rdma(fin.at[pl.ds(pl.multiple_of(other * hh, hh), hh)], fr1, f_send.at[0], f_recv.at[0], part)
     c0.start()
     c0.wait()
-    half[...] = fin[pl.ds(pl.multiple_of(core * hh, hh), hh)] + fr1[...]
+    half = fr1
+    half[...] += fin[pl.ds(pl.multiple_of(core * hh, hh), hh)]
     copies = []
     for i, (c, dev) in enumerate(((zc, zs), (xc, xs), (yc, ys))):
         cp = rdma(half.at[pl.ds(pl.multiple_of(c * qq, qq), qq)], fr2.at[i], f_send.at[1 + i], f_recv.at[1 + i], dev)
@@ -284,37 +388,37 @@
         vm = pl.BlockSpec(memory_space=pltpu.VMEM)
         hb = pl.BlockSpec(memory_space=pl.ANY)
         dma = pltpu.SemaphoreType.DMA
+        tail = feat_rows.T[width // 8 * 8:]
+        tail = jnp.pad(tail, ((0, 8 - tail.shape[0]), (0, 0)))
         with jax.named_scope("gcn"):
             out = pl.pallas_call(
                 functools.partial(kernel, dims),
                 out_shape=jax.ShapeDtypeStruct((fr, hidden), F32),
-                in_specs=[hb, hb, vm, vm, vm, vm],
+                in_specs=[hb, hb, vm, vm, vm, vm, vm],
                 out_specs=vm,
                 scratch_shapes=[
                     pltpu.VMEM((NB, rows, ck), BF),
-                    pltpu.VMEM((20, rows, ck), BF),
+                    pltpu.VMEM((20, ck, rows), BF),
                     pltpu.VMEM((8, 4, hidden, ck), BF),
                     pltpu.VMEM((2, 8, 4, cpad, ck), BF),
                     pltpu.VMEM((2, hidden, rows), F32),
                     pltpu.VMEM((hidden, rows), F32),
                     pltpu.VMEM((2, cpad, rows), F32),
-                    pltpu.VMEM((width, rows), BF),
                     pltpu.VMEM((hidden, rows), BF),
                     pltpu.VMEM((8, 128), F32),
                     pltpu.VMEM((8, 8, 128), F32),
                     pltpu.VMEM((hidden, 128), F32),
                     pltpu.VMEM((fr, hidden), F32),
                     pltpu.VMEM((fr // 2, hidden), F32),
-                    pltpu.VMEM((fr // 2, hidden), F32),
                     pltpu.VMEM((3, fr // 8, hidden), F32),
                     pltpu.VMEM((8, fr // 8, hidden), F32),
-                    dma((NB,)), dma((20,)), dma,
+                    dma((NB,)), dma((2,)),
                     dma((4, 6, 4)), dma((4, 6, 4)), dma((4,)), dma((4,)), dma((8,)), dma((8,)), dma((11,)), dma((11,)),
                 ],
                 compiler_params=pltpu.CompilerParams(
                     collective_id=0, has_side_effects=True, vmem_limit_bytes=67043328
                 ),
-            )(adj_rows, feat_rows.T, w_one, w_two.T, label_rows.reshape(1, rows), mask_rows.reshape(1, rows))
+            )(adj_rows, feat_rows.T, tail, w_one, w_two.T, label_rows.reshape(1, rows), mask_rows.reshape(1, rows))
         return out[w8 + classes, 0], out[:width], out[w8:w8 + classes].T
 
     ax = mesh.axis_names[0]

time: 137 us -> 118 us (0.86)
  Pallas kernels: 132 us -> 111 us
  local copies, waits for them, and re-layouts: 4.24 us -> 5.63 us
    pallas_call x1, Pallas kernels: 132 us -> 111 us  [local_step(): pl.pallas_call(functools.partial(kernel, dims), out_shape=jax.ShapeDtypeS...]
where the time goes in v4:
time: 118 us
  Pallas kernels  111 us (94%)
  local copies, waits for them, and re-layouts  5.63 us (5%)
    pallas_call x1, Pallas kernels, local_step(): pl.pallas_call(functools.partial(kernel, dims), out_shape=jax.ShapeDtypeS...  111 us
    slice x2, local copies, waits for them, and re-layouts, local_step(): return (out[w8 + classes, 0], out[:width], out[w8:w8 + classes].T)  2.89 us

profile of v4, /device:TPU:0, one launch (start us, length us, event | category | flops | bytes accessed | tf_op | source)
XLA Modules:
  0.0 117.6 jit_solution(13640037361645523691)
XLA Ops:
  0.6 0.8 slice.16
  1.4 0.6 pad.4.tail_ref
  2.0 111.4 %gcn.1 = f32[704,128]{1,0:T(8,128)} custom-call(bf16[2048,16384]{1,0:T(8,128)(2,1)} %adj.1, bf16[602,2048]{1,0:T(8,128)(2,1)} %bitcast.8, bf16[8,2048]{1,0:T(8,128)(2,1)} %pad.4.tail_ref, f32[602,128]{1,0:T(8,128)} %w1_ref.1, f32[41,128]{1,0:T(8,128)} %bitcast.9, s32[1,2048]{1,0:T(1,128)} %bitcast.10, s32[1,2048]{1,0:T(1,128)} %bitcast.11), custom_call_target="tpu_custom_call" | custom-call | tf_op jit(solution)/shard_map/gcn/pallas_call | solution.py:394
  113.4 1.2 %slice.13 = f32[1,1]{1,0:T(1,128)} slice(f32[704,128]{1,0:T(8,128)} %gcn.1), slice={[649:650], [0:1]} | slice | bytes 8 | tf_op jit(solution)/shard_map/slice | solution.py:422
  114.6 1.3 %slice_bitcast_fusion = f32[128,41]{0,1:T(8,128)} fusion(f32[704,128]{1,0:T(8,128)} %gcn.1), kind=kLoop, calls=%fused_computation | loop fusion | bytes 41984 | tf_op jit(solution)/shard_map/transpose | solution.py:422
  115.9 1.7 %slice.14 = f32[602,128]{1,0:T(8,128)} slice(f32[704,128]{1,0:T(8,128)} %gcn.1), slice={[0:602], [0:128]} | slice | bytes 616448 | tf_op jit(solution)/shard_map/slice | solution.py:422
